TPU v7x, 128 devices: a whole 4x4x4 slice. The times are simulated.
128 devices in a mesh: sp: 8 (over x, y_lo), ep: 16 (over z, y_hi, core).
Axes of the slice: x: 4, y: 4 (y_hi: 2, y_lo: 2; y = y_hi * 2 + y_lo), z: 4, core: 2. Of those that a mesh axis runs over, the one named last changes fastest.
Arguments:
- residual: bfloat16 [16384, 4096], P(('sp', 'ep')), may hold values from -40 to 40
- queries: bfloat16 [16384, 4096], P(('sp', 'ep')), may hold values from -6 to 6
- key_rows: bfloat16 [16384, 1024], P(('sp', 'ep')), may hold values from -6 to 6
- value_rows: bfloat16 [16384, 1024], P(('sp', 'ep')), may hold values from -6 to 6
- visible: int32 [128, 9], replicated, may hold values from 0 to 1, as said below
- out_proj: bfloat16 [4096, 4096], P(('sp', 'ep')), may hold values from -0.09375 to 0.09375
- norm_gain: float32 [4096], replicated, may hold values from 0.5 to 1.5
- expert_ids: int32 [16384, 2], P(('sp', 'ep')), may hold values from 0 to 7, all different within a row; in each aligned block of 128 rows (0 to 127, 128 to 255, ...) at most 40 rows name the same one
- route_weight: float32 [16384, 2], P(('sp', 'ep')), may hold values from 0.2 to 1
- expert_gate: bfloat16 [2, 7168, 4096], P(None, 'ep'), may hold values from -0.09375 to 0.09375
- expert_up: bfloat16 [2, 7168, 4096], P(None, 'ep'), may hold values from -0.09375 to 0.09375
- expert_down: bfloat16 [2, 7168, 4096], P(None, 'ep'), may hold values from -0.0625 to 0.0625
Outputs:
- layer_out: bfloat16 [16384, 4096], P(('sp', 'ep'))
Inputs may be any that keep to these rules, and one draw needn't show every extreme that they name: The sequence is packed with documents that are runs of whole blocks of 128 tokens, the first of them 9 blocks or longer; visible[q, d] is 1 exactly when block q - d exists and lies in the document of block q, so visible[q, 0] = 1. `expert_ids`: each token names two different experts. Among the 128 tokens of one block no expert is named by more than 40 tokens.
All inputs are finite; a program needn't handle non-finite values.
Results may differ from a plain program's by a relative error of at most 0.0065.
Values may be sent and summed in bfloat16 or wider, within the bound.
No kernel may reach another device: no remote copies, remote signals or barrier semaphores. Data moves between devices by JAX's collectives and lax.ppermute only.
A program may use at most 128 MiB of HBM per device.

v0:
```python
import math
import jax
import jax.numpy as jnp
from jax import lax
from jax.sharding import Mesh
from jax.sharding import PartitionSpec as P

HEAD = 128
CAP = 40
SP = ("sp_0", "sp_1")
EP = ("ep_0", "ep_1", "ep_2")
SP_EP = ("sp_0", "sp_1", "ep_0", "ep_1", "ep_2")


def shifted(value, axis, steps):
    count = lax.axis_size(axis)
    pairs = [(source, (source + steps) % count) for source in range(count)]
    return lax.ppermute(value, axis, pairs)


def sum_by_axis(terms, axes):
    total = terms.astype(jnp.bfloat16)
    for axis in axes:
        total = lax.psum_scatter(total, axis, scatter_dimension=0, tiled=True)
    return total.astype(jnp.float32)


def split_up(array, dim, size):
    before, after = (array.shape[:dim], array.shape[dim + 1 :])
    return jnp.moveaxis(array.reshape(*before, size, -1, *after), dim, 0)


def summed_rows(array, chips, core, dim):
    sizes = (lax.axis_size(chips), lax.axis_size(core))
    blocks = split_up(array, dim, sizes[0] * sizes[1])
    inside = blocks.shape[1:]
    blocks = blocks.reshape(*sizes, *inside).swapaxes(0, 1).reshape(-1, *inside)
    blocks = lax.psum_scatter(blocks, core, scatter_dimension=0, tiled=True)
    return lax.psum_scatter(blocks, chips, scatter_dimension=0, tiled=True)[0]


def settle(shard_piece, distance, ep_index):
    lowered = jnp.concatenate([jnp.zeros_like(shard_piece[:1]), shard_piece[:-1]], axis=0)
    return jnp.where(distance > ep_index, lowered, shard_piece)


def local(
    residual,
    queries,
    key_rows,
    value_rows,
    visible,
    out_proj,
    norm_gain,
    expert_ids,
    route_weight,
    expert_gate,
    expert_up,
    expert_down,
):
    sp_count = lax.axis_size(SP)
    ep_count = lax.axis_size(EP)
    ep_index = lax.axis_index(EP)
    tokens = residual.shape[0]
    reach = ep_count // 2 + 1
    query_width = queries.shape[1] // sp_count
    key_width = key_rows.shape[1] // sp_count
    key_heads = key_width // HEAD
    grouping = query_width // key_width
    query_send = queries.reshape(1, tokens, sp_count, query_width)
    key_send = key_rows.reshape(1, tokens, sp_count, key_width)
    value_send = value_rows.reshape(1, tokens, sp_count, key_width)
    query_heads, key_local, value_local = (
        lax.all_to_all(query_send, SP, split_axis=2, concat_axis=0, tiled=True),
        lax.all_to_all(key_send, SP, split_axis=2, concat_axis=0, tiled=True),
        lax.all_to_all(value_send, SP, split_axis=2, concat_axis=0, tiled=True),
    )
    key_value = jnp.concatenate(
        [
            key_local.reshape(sp_count, tokens, key_width),
            value_local.reshape(sp_count, tokens, key_width),
        ],
        axis=2,
    )
    pieces = [key_value]
    for distance in range(1, reach):
        pieces.append(settle(shifted(key_value, EP, distance), distance, ep_index))
    window = jnp.stack(pieces, axis=0)
    key_window = window[..., :key_width].reshape(reach, sp_count, tokens, key_heads, HEAD)
    value_window = window[..., key_width:].reshape(reach, sp_count, tokens, key_heads, HEAD)
    query_local = query_heads.reshape(sp_count, tokens, key_heads, grouping, HEAD)
    scores = jnp.einsum(
        "stgrh,dsugh->sgrtdu", query_local, key_window, preferred_element_type=jnp.float32
    ) * (1.0 / math.sqrt(HEAD))
    seen = lax.dynamic_index_in_dim(
        visible.reshape(sp_count, ep_count, reach), ep_index, 1, keepdims=False
    )
    position = jnp.arange(tokens)
    distances = jnp.arange(reach)
    allowed = (seen[:, None, :, None] > 0) & (
        (distances[None, None, :, None] > 0)
        | (position[None, None, None, :] <= position[None, :, None, None])
    )
    allowed = allowed[:, None, None]
    scores = jnp.where(allowed, scores, -1e30)
    peak = jnp.max(scores, axis=(4, 5), keepdims=True)
    weights_f = jnp.where(allowed, jnp.exp(scores - peak), 0.0)
    totals = jnp.sum(weights_f, axis=(4, 5))
    weights_b = weights_f.astype(jnp.bfloat16)
    summed = jnp.einsum(
        "sgrtdu,dsugh->stgrh", weights_b, value_window, preferred_element_type=jnp.float32
    )
    attended = (summed / jnp.transpose(totals, (0, 3, 1, 2))[..., None]).astype(jnp.bfloat16)
    attended = attended.reshape(sp_count * tokens, query_width)
    proj_full = lax.all_gather(out_proj, EP, axis=0, tiled=True)
    projected = sum_by_axis(jnp.dot(attended, proj_full, preferred_element_type=jnp.float32), SP)
    hidden_sum = residual.astype(jnp.float32) + projected
    mean_square = jnp.mean(hidden_sum * hidden_sum, axis=-1, keepdims=True)
    normed = (hidden_sum * lax.rsqrt(mean_square + 1e-05) * norm_gain).astype(jnp.bfloat16)
    window_experts = expert_gate.shape[0]
    capacity = CAP
    choose = expert_ids[None] == jnp.arange(window_experts, dtype=jnp.int32)[:, None, None]
    member = jnp.any(choose, axis=2)
    token_weight = jnp.sum(jnp.where(choose, route_weight[None], 0.0), axis=2)
    ranked = jnp.cumsum(member.astype(jnp.int32), axis=1) - member.astype(jnp.int32)
    slot_hit = (
        ranked[:, None, :] == jnp.arange(capacity, dtype=jnp.int32)[None, :, None]
    ) & member[:, None, :]
    dispatch = slot_hit.astype(jnp.bfloat16)
    outgoing = jnp.einsum(
        "wct,td->wcd", dispatch, normed, preferred_element_type=jnp.float32
    ).astype(jnp.bfloat16)
    combine = jnp.where(slot_hit, token_weight[:, None, :], 0.0)
    shard_piece = lax.all_gather(outgoing, EP, axis=1, tiled=True)
    gate_act = jnp.einsum(
        "wnd,wfd->wnf", shard_piece, expert_gate, preferred_element_type=jnp.float32
    )
    up_act = jnp.einsum("wnd,wfd->wnf", shard_piece, expert_up, preferred_element_type=jnp.float32)
    activated = (jax.nn.silu(gate_act) * up_act).astype(jnp.bfloat16)
    partial_value = jnp.einsum(
        "wnf,wfd->wnd", activated, expert_down, preferred_element_type=jnp.float32
    )
    returned = summed_rows(partial_value.astype(jnp.bfloat16), ("ep_0", "ep_1"), "ep_2", 1).astype(
        jnp.float32
    )
    expert_mix = jnp.einsum("wct,wcd->td", combine, returned, precision=lax.Precision.HIGHEST)
    return (hidden_sum + expert_mix).astype(jnp.bfloat16)


def solution(mesh):
    finer = Mesh(mesh.devices.reshape(4, 2, 4, 2, 2), ("sp_0", "sp_1", "ep_0", "ep_1", "ep_2"))
    in_specs = (
        P(SP_EP, None),
        P(SP_EP, None),
        P(SP_EP, None),
        P(SP_EP, None),
        P(),
        P(SP_EP, None),
        P(),
        P(SP_EP, None),
        P(SP_EP, None),
        P(None, EP, None),
        P(None, EP, None),
        P(None, EP, None),
    )
    out_specs = P(SP_EP, None)
    return jax.shard_map(local, mesh=finer, in_specs=in_specs, out_specs=out_specs, check_vma=False)
```

profile of v0, /device:TPU:0, one launch (start us, length us, event | category | flops | bytes accessed | tf_op | source)
XLA Modules:
  0.0 554.0 jit_solution(9617605456632992405)
XLA Ops:
  6.5 1.1 copy.87
  7.7 0.9 copy.88
  8.5 5.4 all-to-all-start
  13.9 1.1 copy.89
  15.1 0.9 copy.90
  15.9 5.2 all-to-all-done
  21.2 3.4 all-to-all-start.1
  24.6 0.7 all-gather.3.cloned.1.call-update
  25.3 0.8 reshape.128
  26.1 2.3 copy.100
  28.4 3.1 all-to-all-done.1
  31.4 4.2 all-to-all-start.2
  35.7 0.9 pad_maximum_fusion
  36.6 2.9 collective-permute-start.1
  39.5 4.3 collective-permute-start.2
  43.8 0.1 constant_dynamic-slice_fusion
  43.9 0.1 copy.116
  44.1 0.1 broadcast_or_fusion
  44.2 2.0 collective-permute-start.3
  46.2 18.2 %collective-permute-done = bf16[8,128,256]{2,1,0:T(8,128)(2,1)S(1)} collective-permute-done((bf16[8,128,256]{2,1,0:T(8,128)(2,1)}, bf16[8,128,256]{2,1,0:T(8,128)(2,1)S(1)}, u32[]{:S(2)}, u32[]{:S(2)}) %collective-permute-start) | collective-permute-done | bytes 524320 | tf_op jit(solution)/shard_map/ppermute | solution.py:18
  64.4 2.3 collective-permute-done.1
  66.7 8.3 %collective-permute-start.6 = (bf16[8,128,256]{2,1,0:T(8,128)(2,1)}, bf16[8,128,256]{2,1,0:T(8,128)(2,1)}, u32[]{:S(2)}, u32[]{:S(2)}) collective-permute-start(bf16[8,128,256]{2,1,0:T(8,128)(2,1)} %pad_maximum_fusion), channel_id=1, source_target_pairs={{0,7},{1,8},{2,9},{3,10},{4,11},{5,12},{6,13},{7,14},{8,15},{9,0},... | collective-permute-start | bytes 1572872 | tf_op jit(solution)/shard_map/ppermute | solution.py:18
  75.0 25.7 %collective-permute-done.2 = bf16[8,128,256]{2,1,0:T(8,128)(2,1)S(1)} collective-permute-done((bf16[8,128,256]{2,1,0:T(8,128)(2,1)}, bf16[8,128,256]{2,1,0:T(8,128)(2,1)S(1)}, u32[]{:S(2)}, u32[]{:S(2)}) %collective-permute-start.2) | collective-permute-done | bytes 524320 | tf_op jit(solution)/shard_map/ppermute | solution.py:18
  100.7 0.6 broadcast_and_fusion
  101.4 0.8 bitcast_dynamic-update-slice_fusion.7
  102.3 5.5 collective-permute-done.3
  107.8 1.0 slice.43
  108.9 8.1 %collective-permute-done.4 = bf16[8,128,256]{2,1,0:T(8,128)(2,1)} collective-permute-done((bf16[8,128,256]{2,1,0:T(8,128)(2,1)}, bf16[8,128,256]{2,1,0:T(8,128)(2,1)}, u32[]{:S(2)}, u32[]{:S(2)}) %collective-permute-start.4) | collective-permute-done | bytes 524320 | tf_op jit(solution)/shard_map/ppermute | solution.py:18
  117.0 1.0 slice.44
  118.0 1.0 slice.45
  119.1 5.4 collective-permute-done.6
  124.5 1.0 slice.46
  125.5 9.7 %collective-permute-done.7 = bf16[8,128,256]{2,1,0:T(8,128)(2,1)} collective-permute-done((bf16[8,128,256]{2,1,0:T(8,128)(2,1)}, bf16[8,128,256]{2,1,0:T(8,128)(2,1)}, u32[]{:S(2)}, u32[]{:S(2)}) %collective-permute-start.7) | collective-permute-done | bytes 524320 | tf_op jit(solution)/shard_map/ppermute | solution.py:18
  135.2 1.1 slice.47
  136.2 0.9 bitcast_dynamic-update-slice_fusion.6
  137.1 0.9 bitcast_dynamic-update-slice_fusion.5
  138.1 0.9 bitcast_dynamic-update-slice_fusion.4
  139.0 0.9 bitcast_dynamic-update-slice_fusion.3
  139.9 0.9 bitcast_dynamic-update-slice_fusion.2
  140.8 0.9 bitcast_dynamic-update-slice_fusion.1
  141.8 0.9 bitcast_dynamic-update-slice_fusion
  142.7 0.9 bitcast_dynamic-update-slice_fusion.8
  143.6 4.8 fusion
  148.4 5.0 fusion.1
  153.4 1.5 copy-done
  154.9 9.7 %fusion.10 = bf16[8,128,1,4,128]{1,4,3,0,2:T(8,128)(2,1)S(1)} fusion(f32[8,9,128,128,4]{3,2,4,1,0:T(8,128)} %copy-done, f32[8,4,128]{2,1,0:T(4,128)S(1)} %get-tuple-element.5, pred[8,128,9,128]{1,3,2,0:T(8,128)(4,1)S(1)} %broadcast_and_fusion, bf16[9,8,128,256]{3,2,0,1:T(8,128)(2,1)} %bitcast_dynamic-update-slice_fusion.8, f32[8,128,4]{1,2,0:T(4,128)S(1)} %bitcast.157), kind=kOutput, calls=%fused_computation.20 | convolution fusion | flops 1232601088 | bytes 23494656 | tf_op jit(solution)/shard_map/sgrtdu,dsugh->stgrh/dot_general | solution.py:110
  164.6 0.7 copy.104
  165.3 9.0 %convolution_convert_fusion.1 = bf16[1024,4096]{1,0:T(8,128)(2,1)} fusion(bf16[512,4096]{1,0:T(8,128)(2,1)} %all-gather.3.cloned.1.call-done, bf16[64,8,8,128]{3,2,1,0:T(8,128)(2,1)S(1)} %bitcast.154), kind=kOutput, calls=%fused_computation.9 | convolution fusion | flops 4299161600 | bytes 13631488 | tf_op jit(solution)/shard_map/dot_general | solution.py:116
  174.4 0.0 reduce-scatter.7.cloned.1.call-start
  174.4 85.9 %reduce-scatter.5.cloned.1.call-done = bf16[256,4096]{1,0:T(8,128)(2,1)} async-done(((bf16[1024,4096]{1,0:T(8,128)(2,1)}), bf16[256,4096]{1,0:T(8,128)(2,1)}) %reduce-scatter.5.cloned.1.call-update) | async-done | bytes 2097168 | tf_op jit(solution)/shard_map/reduce_scatter | solution.py:24
  260.5 0.3 reduce_window_sum.11
  260.8 36.1 %reduce-scatter.7.cloned.1.call-done = bf16[128,4096]{1,0:T(8,128)(2,1)} async-done(((bf16[256,4096]{1,0:T(8,128)(2,1)}), bf16[128,4096]{1,0:T(8,128)(2,1)}) %reduce-scatter.7.cloned.1.call-update) | async-done | bytes 1048592 | tf_op jit(solution)/shard_map/reduce_scatter | solution.py:24
  296.9 1.6 multiply_reduce_fusion
  298.6 2.7 convolution_convert_fusion.2
  301.3 0.3 reduce-scatter.9.cloned.1.call-start
  301.6 82.6 %all-gather.5.cloned.1.call-done = bf16[2,640,4096]{2,1,0:T(8,128)(2,1)} async-done(((bf16[2,40,4096]{2,1,0:T(8,128)(2,1)}), bf16[2,640,4096]{2,1,0:T(8,128)(2,1)}) %all-gather.5.cloned.1.call-update) | async-done | bytes 10485776 | tf_op jit(solution)/shard_map/all_gather | solution.py:134
  384.1 13.0 %fusion.35 = f32[2,640,448]{1,2,0:T(8,128)} fusion(bf16[2,640,4096]{2,1,0:T(8,128)(2,1)} %all-gather.5.cloned.1.call-done, bf16[2,448,4096]{2,1,0:T(8,128)(2,1)} %param.21), kind=kOutput, calls=%fused_computation.63 | convolution fusion | flops 4697620480 | bytes 20119552 | tf_op jit(solution)/shard_map/wnd,wfd->wnf/dot_general | solution.py:135
  397.1 12.4 %multiply_convert_fusion = bf16[2,640,448]{1,2,0:T(8,128)(2,1)S(1)} fusion(f32[2,640,448]{1,2,0:T(8,128)} %fusion.35, bf16[2,640,4096]{2,1,0:T(8,128)(2,1)} %all-gather.5.cloned.1.call-done, bf16[2,448,4096]{2,1,0:T(8,128)(2,1)} %param.22), kind=kOutput, calls=%fused_computation.18 | convolution fusion | flops 4701061120 | bytes 21266432 | tf_op jit(solution)/shard_map/wnd,wfd->wnf/dot_general | solution.py:138
  409.5 10.2 %convolution_convert_fusion = bf16[2,640,4096]{2,1,0:T(8,128)(2,1)} fusion(bf16[2,640,448]{1,2,0:T(8,128)(2,1)S(1)} %multiply_convert_fusion, bf16[2,448,4096]{2,1,0:T(8,128)(2,1)} %param.23), kind=kOutput, calls=%fused_computation.8 | convolution fusion | flops 4702863360 | bytes 18972672 | tf_op jit(solution)/shard_map/wnf,wfd->wnd/dot_general | solution.py:140
  419.7 9.6 %copy.105 = bf16[8,2,2,40,4096]{4,3,2,0,1:T(8,128)(2,1)} copy(bf16[8,2,2,40,4096]{4,3,1,0,2:T(8,128)(2,1)} %bitcast.149) | data formatting | bytes 20971520 | tf_op jit(solution)/shard_map/reshape | solution.py:37
  429.4 0.0 reduce-scatter.11.cloned.1.call-start
  429.4 18.5 %reduce-scatter.9.cloned.1.call-done = bf16[8,2,40,4096]{3,2,1,0:T(8,128)(2,1)} async-done(((bf16[16,2,40,4096]{3,2,1,0:T(8,128)(2,1)}), bf16[8,2,40,4096]{3,2,1,0:T(8,128)(2,1)}) %reduce-scatter.9.cloned.1.call-update) | async-done | bytes 5242896 | tf_op jit(solution)/shard_map/reduce_scatter | solution.py:38
  448.0 95.9 %reduce-scatter.11.cloned.1.call-done = bf16[1,2,40,4096]{3,2,1,0:T(8,128)(2,1)} async-done(((bf16[8,2,40,4096]{3,2,1,0:T(8,128)(2,1)}), bf16[1,2,40,4096]{3,2,1,0:T(8,128)(2,1)}) %reduce-scatter.11.cloned.1.call-update) | async-done | bytes 655376 | tf_op jit(solution)/shard_map/reduce_scatter | solution.py:39
  543.9 3.2 fusion.8
  (37 shorter events, 0.4 us)
Async XLA Ops:
  8.5 12.6 %all-to-all-start = ((bf16[1,128,8,128]{3,1,0,2:T(8,128)(2,1)}), bf16[1,128,8,128]{3,1,0,2:T(8,128)(2,1)S(1)}, u32[]{:S(2)}, u32[]{:S(2)}) async-start(bf16[1,128,8,128]{3,1,0,2:T(8,128)(2,1)} %copy.88), calls=%async_computation | async-start | bytes 524288 | tf_op jit(solution)/shard_map/all_to_all | solution.py:75
  21.2 10.3 %all-to-all-start.1 = ((bf16[1,128,8,128]{3,1,0,2:T(8,128)(2,1)}), bf16[1,128,8,128]{3,1,0,2:T(8,128)(2,1)S(1)}, u32[]{:S(2)}, u32[]{:S(2)}) async-start(bf16[1,128,8,128]{3,1,0,2:T(8,128)(2,1)} %copy.90), calls=%async_computation.1 | async-start | bytes 524288 | tf_op jit(solution)/shard_map/all_to_all | solution.py:76
  24.6 140.7 %all-gather.3.cloned.1.call-start = ((), (), s32[]{:S(2)}) async-start(), calls=%async_computation.7 | async-start | bytes 4456448 | tf_op jit(solution)/shard_map/all_gather | solution.py:115
  31.4 112.2 %all-to-all-start.2 = ((bf16[1,128,8,512]{1,3,0,2:T(8,128)(2,1)}), bf16[1,128,8,512]{1,3,0,2:T(8,128)(2,1)}, u32[]{:S(2)}, u32[]{:S(2)}) async-start(bf16[1,128,8,512]{1,3,0,2:T(8,128)(2,1)} %bitcast.29), calls=%async_computation.2 | async-start | bytes 2097152 | tf_op jit(solution)/shard_map/all_to_all | solution.py:74
  35.7 224.7 %reduce-scatter.5.cloned.1.call-start = ((), (), s32[]{:S(2)}) async-start(), calls=%async_computation.8 | async-start | bytes 10485760 | tf_op jit(solution)/shard_map/reduce_scatter | solution.py:24
  36.6 27.8 %collective-permute-start = (bf16[8,128,256]{2,1,0:T(8,128)(2,1)}, bf16[8,128,256]{2,1,0:T(8,128)(2,1)S(1)}, u32[]{:S(2)}, u32[]{:S(2)}) collective-permute-start(bf16[8,128,256]{2,1,0:T(8,128)(2,1)} %pad_maximum_fusion), channel_id=1, source_target_pairs={{0,1},{1,2},{2,3},{3,4},{4,5},{5,6},{6,7},{7,8},{8,9},{9,10},{10,1... | collective-permute-start | bytes 1572872 | tf_op jit(solution)/shard_map/ppermute | solution.py:18
  36.6 30.1 %collective-permute-start.1 = (bf16[8,128,256]{2,1,0:T(8,128)(2,1)}, bf16[8,128,256]{2,1,0:T(8,128)(2,1)S(1)}, u32[]{:S(2)}, u32[]{:S(2)}) collective-permute-start(bf16[8,128,256]{2,1,0:T(8,128)(2,1)} %pad_maximum_fusion), channel_id=1, source_target_pairs={{0,2},{1,3},{2,4},{3,5},{4,6},{5,7},{6,8},{7,9},{8,10},{9,11},{10,... | collective-permute-start | bytes 1572872 | tf_op jit(solution)/shard_map/ppermute | solution.py:18
  39.5 61.2 %collective-permute-start.2 = (bf16[8,128,256]{2,1,0:T(8,128)(2,1)}, bf16[8,128,256]{2,1,0:T(8,128)(2,1)S(1)}, u32[]{:S(2)}, u32[]{:S(2)}) collective-permute-start(bf16[8,128,256]{2,1,0:T(8,128)(2,1)} %pad_maximum_fusion), channel_id=1, source_target_pairs={{0,3},{1,4},{2,5},{3,6},{4,7},{5,8},{6,9},{7,10},{8,11},{9,12},{10... | collective-permute-start | bytes 1572872 | tf_op jit(solution)/shard_map/ppermute | solution.py:18
  44.2 63.6 %collective-permute-start.3 = (bf16[8,128,256]{2,1,0:T(8,128)(2,1)}, bf16[8,128,256]{2,1,0:T(8,128)(2,1)}, u32[]{:S(2)}, u32[]{:S(2)}) collective-permute-start(bf16[8,128,256]{2,1,0:T(8,128)(2,1)} %pad_maximum_fusion), channel_id=1, source_target_pairs={{0,4},{1,5},{2,6},{3,7},{4,8},{5,9},{6,10},{7,11},{8,12},{9,13},{1... | collective-permute-start | bytes 1572872 | tf_op jit(solution)/shard_map/ppermute | solution.py:18
  46.2 70.8 %collective-permute-start.4 = (bf16[8,128,256]{2,1,0:T(8,128)(2,1)}, bf16[8,128,256]{2,1,0:T(8,128)(2,1)}, u32[]{:S(2)}, u32[]{:S(2)}) collective-permute-start(bf16[8,128,256]{2,1,0:T(8,128)(2,1)} %pad_maximum_fusion), channel_id=1, source_target_pairs={{0,5},{1,6},{2,7},{3,8},{4,9},{5,10},{6,11},{7,12},{8,13},{9,14},{... | collective-permute-start | bytes 1572872 | tf_op jit(solution)/shard_map/ppermute | solution.py:18
  64.4 53.6 %collective-permute-start.5 = (bf16[8,128,256]{2,1,0:T(8,128)(2,1)}, bf16[8,128,256]{2,1,0:T(8,128)(2,1)}, u32[]{:S(2)}, u32[]{:S(2)}) collective-permute-start(bf16[8,128,256]{2,1,0:T(8,128)(2,1)} %pad_maximum_fusion), channel_id=1, source_target_pairs={{0,6},{1,7},{2,8},{3,9},{4,10},{5,11},{6,12},{7,13},{8,14},{9,15},... | collective-permute-start | bytes 1572872 | tf_op jit(solution)/shard_map/ppermute | solution.py:18
  66.7 57.7 %collective-permute-start.6 = (bf16[8,128,256]{2,1,0:T(8,128)(2,1)}, bf16[8,128,256]{2,1,0:T(8,128)(2,1)}, u32[]{:S(2)}, u32[]{:S(2)}) collective-permute-start(bf16[8,128,256]{2,1,0:T(8,128)(2,1)} %pad_maximum_fusion), channel_id=1, source_target_pairs={{0,7},{1,8},{2,9},{3,10},{4,11},{5,12},{6,13},{7,14},{8,15},{9,0},... | collective-permute-start | bytes 1572872 | tf_op jit(solution)/shard_map/ppermute | solution.py:18
  100.7 34.5 %collective-permute-start.7 = (bf16[8,128,256]{2,1,0:T(8,128)(2,1)}, bf16[8,128,256]{2,1,0:T(8,128)(2,1)}, u32[]{:S(2)}, u32[]{:S(2)}) collective-permute-start(bf16[8,128,256]{2,1,0:T(8,128)(2,1)} %pad_maximum_fusion), channel_id=1, source_target_pairs={{0,8},{1,9},{2,10},{3,11},{4,12},{5,13},{6,14},{7,15},{8,0},{9,1},... | collective-permute-start | bytes 1572872 | tf_op jit(solution)/shard_map/ppermute | solution.py:18
  148.4 6.5 %copy-start = (f32[8,9,128,128,4]{3,2,4,1,0:T(8,128)}, f32[8,9,128,128,4]{3,2,4,1,0:T(8,128)S(1)}, u32[]{:S(2)}) copy-start(f32[8,9,128,128,4]{3,2,4,1,0:T(8,128)S(1)} %get-tuple-element.6) | copy-start | bytes 56623108
  174.3 86.1 %copy-start.4 = (s32[128,2]{0,1:T(2,128)S(1)}, s32[128,2]{0,1:T(2,128)}, u32[]{:S(2)}) copy-start(s32[128,2]{0,1:T(2,128)} %param.19) | copy-start | bytes 3076
  174.3 122.6 %copy-start.1 = (bf16[128,4096]{1,0:T(8,128)(2,1)S(1)}, bf16[128,4096]{1,0:T(8,128)(2,1)}, u32[]{:S(2)}) copy-start(bf16[128,4096]{1,0:T(8,128)(2,1)} %param.12) | copy-start | bytes 3145732
  174.3 124.2 %copy-start.3 = (f32[4096]{0:T(1024)S(1)}, f32[4096]{0:T(1024)}, u32[]{:S(2)}) copy-start(f32[4096]{0:T(1024)} %param.18) | copy-start | bytes 49156
  174.4 122.6 %reduce-scatter.7.cloned.1.call-start = ((), (), s32[]{:S(2)}) async-start(), calls=%async_computation.9 | async-start | bytes 3145728 | tf_op jit(solution)/shard_map/reduce_scatter | solution.py:24
  260.4 123.7 %all-gather.5.cloned.1.call-start = ((), (), s32[]{:S(2)}) async-start(), calls=%async_computation.10 | async-start | bytes 11141120 | tf_op jit(solution)/shard_map/all_gather | solution.py:134
  301.3 146.6 %reduce-scatter.9.cloned.1.call-start = ((), (), s32[]{:S(2)}) async-start(), calls=%async_computation.11 | async-start | bytes 15728640 | tf_op jit(solution)/shard_map/reduce_scatter | solution.py:38
  429.3 18.6 %copy-start.5 = (f32[128,2]{0,1:T(2,128)S(1)}, f32[128,2]{0,1:T(2,128)}, u32[]{:S(2)}) copy-start(f32[128,2]{0,1:T(2,128)} %param.20) | copy-start | bytes 3076
  429.4 114.6 %copy-start.2 = (bf16[128,4096]{1,0:T(8,128)(2,1)S(1)}, bf16[128,4096]{1,0:T(8,128)(2,1)}, u32[]{:S(2)}) copy-start(bf16[128,4096]{1,0:T(8,128)(2,1)} %reduce-scatter.7.cloned.1.call-done) | copy-start | bytes 3145732
  429.4 114.6 %reduce-scatter.11.cloned.1.call-start = ((), (), s32[]{:S(2)}) async-start(), calls=%async_computation.12 | async-start | bytes 5898240 | tf_op jit(solution)/shard_map/reduce_scatter | solution.py:39
Sparse Core Ops, SparseCore 0:
  27.8 117.8 all-gather.2
  174.5 85.8 reduce-scatter.4
  262.7 34.1 reduce-scatter.6
  301.4 82.6 all-gather.4
  429.5 18.4 reduce-scatter.8
  451.6 92.2 reduce-scatter.10
where the time goes:
time: 555 us; the launch traced here: 554 us
  waiting for transfers between devices  403 us (73%)
  matrix products  64.9 us (12%)
  starting transfers between devices  31 us (6%)
  local copies, waits for them, and re-layouts  24.3 us (4%)
  other arithmetic  16.9 us (3%)
  between operations  13.7 us (2%)
    reduce_scatter x2, waiting for transfers between devices, sum_by_axis(): total = lax.psum_scatter(total, axis, scatter_dimension=0, tiled=True)  122 us
    reduce_scatter x1, waiting for transfers between devices, summed_rows(): return lax.psum_scatter(blocks, chips, scatter_dimension=0, tiled=True)[0]  95.9 us
    all_gather x1, waiting for transfers between devices, local(): shard_piece = lax.all_gather(outgoing, EP, axis=1, tiled=True)  82.6 us
    ppermute x8, waiting for transfers between devices, shifted(): return lax.ppermute(value, axis, pairs)  74.9 us
    reduce_scatter x1, waiting for transfers between devices, summed_rows(): blocks = lax.psum_scatter(blocks, core, scatter_dimension=0, tiled=True)  18.5 us
    ppermute x8, starting transfers between devices, shifted(): return lax.ppermute(value, axis, pairs)  17.5 us
    dot_general x1, matrix products, local(): jnp.einsum('wnd,wfd->wnf', shard_piece, expert_gate, preferred_element_ty...  13 us
    dot_general x1, matrix products, local(): jnp.einsum('wnd,wfd->wnf', shard_piece, expert_up, preferred_element_type...  12.4 us
  transfers between devices with their start and end apart: 17, of which 14 were waited for; matrix products, arithmetic and copies ran while one was open for 7% of the time, Pallas kernels for 0%

commit v1 on v0

--- a/solution.py
+++ b/solution.py
@@ -131,7 +131,8 @@
         "wct,td->wcd", dispatch, normed, preferred_element_type=jnp.float32
     ).astype(jnp.bfloat16)
     combine = jnp.where(slot_hit, token_weight[:, None, :], 0.0)
-    shard_piece = lax.all_gather(outgoing, EP, axis=1, tiled=True)
+    sent = jnp.stack([outgoing] * lax.axis_size(EP))
+    shard_piece = jnp.concatenate(lax.all_to_all(sent, EP, 0, 0), axis=1)
     gate_act = jnp.einsum(
         "wnd,wfd->wnf", shard_piece, expert_gate, preferred_element_type=jnp.float32
     )

time: 555 us -> 608 us (1.095)
  blocking collectives: 0 us -> 126 us
  waiting for transfers between devices: 403 us -> 320 us
  local copies, waits for them, and re-layouts: 24.3 us -> 35.1 us
    all_to_all x0 -> x1, blocking collectives: none -> 126 us  [local(): shard_piece = jnp.concatenate(lax.all_to_all(sent, EP, 0, 0), axis=1)]
    all_gather x1 -> x0, waiting for transfers between devices: 82.6 us -> none  [local(): shard_piece = lax.all_gather(outgoing, EP, axis=1, tiled=True)]
    reshape x0 -> x1, local copies, waits for them, and re-layouts: none -> 9.59 us  [local(): shard_piece = jnp.concatenate(lax.all_to_all(sent, EP, 0, 0), axis=1)]
  transfers between devices with their start and end apart: 17 -> 16, of which waited for: 14 -> 13; matrix products, arithmetic and copies ran while one was open for 7% -> 7% of each run, Pallas kernels for 0% -> 0%
where the time goes in v1:
time: 608 us; the launch traced here: 607 us
  waiting for transfers between devices  320 us (53%)
  blocking collectives  126 us (21%)
  matrix products  65.6 us (11%)
  local copies, waits for them, and re-layouts  35.1 us (6%)
  starting transfers between devices  30.8 us (5%)
  other arithmetic  16.9 us (3%)
  between operations  13.4 us (2%)
    all_to_all x1, blocking collectives, local(): shard_piece = jnp.concatenate(lax.all_to_all(sent, EP, 0, 0), axis=1)  126 us
    reduce_scatter x2, waiting for transfers between devices, sum_by_axis(): total = lax.psum_scatter(total, axis, scatter_dimension=0, tiled=True)  122 us
    reduce_scatter x1, waiting for transfers between devices, summed_rows(): return lax.psum_scatter(blocks, chips, scatter_dimension=0, tiled=True)[0]  95.9 us
    ppermute x8, waiting for transfers between devices, shifted(): return lax.ppermute(value, axis, pairs)  74.9 us
    reduce_scatter x1, waiting for transfers between devices, summed_rows(): blocks = lax.psum_scatter(blocks, core, scatter_dimension=0, tiled=True)  17.7 us
    ppermute x8, starting transfers between devices, shifted(): return lax.ppermute(value, axis, pairs)  17.5 us
    dot_general x1, matrix products, local(): jnp.einsum('wnd,wfd->wnf', shard_piece, expert_gate, preferred_element_ty...  13.5 us
    dot_general x1, matrix products, local(): jnp.einsum('wnd,wfd->wnf', shard_piece, expert_up, preferred_element_type...  12.9 us
  transfers between devices with their start and end apart: 16, of which 13 were waited for; matrix products, arithmetic and copies ran while one was open for 7% of the time, Pallas kernels for 0%

profile of v1, /device:TPU:0, one launch (start us, length us, event | category | flops | bytes accessed | tf_op | source)
XLA Modules:
  0.0 607.1 jit_solution(11504001402883737889)
XLA Ops:
  6.5 1.1 copy.89
  7.7 0.9 copy.90
  8.5 5.4 all-to-all-start
  13.9 1.1 copy.91
  15.1 0.9 copy.92
  15.9 5.2 all-to-all-done
  21.2 3.4 all-to-all-start.1
  24.6 0.7 all-gather.2.cloned.1.call-update
  25.3 0.8 reshape.136
  26.1 2.3 copy.102
  28.4 3.1 all-to-all-done.1
  31.4 4.2 all-to-all-start.2
  35.7 0.8 pad_maximum_fusion
  36.6 2.9 collective-permute-start.1
  39.5 4.3 collective-permute-start.2
  43.8 0.1 constant_dynamic-slice_fusion
  43.9 0.1 copy.119
  44.1 0.1 broadcast_or_fusion
  44.2 2.0 collective-permute-start.3
  46.2 18.2 %collective-permute-done = bf16[8,128,256]{2,1,0:T(8,128)(2,1)S(1)} collective-permute-done((bf16[8,128,256]{2,1,0:T(8,128)(2,1)}, bf16[8,128,256]{2,1,0:T(8,128)(2,1)S(1)}, u32[]{:S(2)}, u32[]{:S(2)}) %collective-permute-start) | collective-permute-done | bytes 524320 | tf_op jit(solution)/shard_map/ppermute | solution.py:18
  64.4 2.3 collective-permute-done.1
  66.7 8.3 %collective-permute-start.6 = (bf16[8,128,256]{2,1,0:T(8,128)(2,1)}, bf16[8,128,256]{2,1,0:T(8,128)(2,1)}, u32[]{:S(2)}, u32[]{:S(2)}) collective-permute-start(bf16[8,128,256]{2,1,0:T(8,128)(2,1)} %pad_maximum_fusion), channel_id=1, source_target_pairs={{0,7},{1,8},{2,9},{3,10},{4,11},{5,12},{6,13},{7,14},{8,15},{9,0},... | collective-permute-start | bytes 1572872 | tf_op jit(solution)/shard_map/ppermute | solution.py:18
  75.0 25.7 %collective-permute-done.2 = bf16[8,128,256]{2,1,0:T(8,128)(2,1)S(1)} collective-permute-done((bf16[8,128,256]{2,1,0:T(8,128)(2,1)}, bf16[8,128,256]{2,1,0:T(8,128)(2,1)S(1)}, u32[]{:S(2)}, u32[]{:S(2)}) %collective-permute-start.2) | collective-permute-done | bytes 524320 | tf_op jit(solution)/shard_map/ppermute | solution.py:18
  100.7 0.6 broadcast_and_fusion
  101.3 0.9 bitcast_dynamic-update-slice_fusion.7
  102.3 5.5 collective-permute-done.3
  107.8 1.0 slice.43
  108.9 8.1 %collective-permute-done.4 = bf16[8,128,256]{2,1,0:T(8,128)(2,1)} collective-permute-done((bf16[8,128,256]{2,1,0:T(8,128)(2,1)}, bf16[8,128,256]{2,1,0:T(8,128)(2,1)}, u32[]{:S(2)}, u32[]{:S(2)}) %collective-permute-start.4) | collective-permute-done | bytes 524320 | tf_op jit(solution)/shard_map/ppermute | solution.py:18
  117.0 1.0 slice.44
  118.0 1.0 slice.45
  119.1 5.4 collective-permute-done.6
  124.5 1.0 slice.46
  125.5 9.7 %collective-permute-done.7 = bf16[8,128,256]{2,1,0:T(8,128)(2,1)} collective-permute-done((bf16[8,128,256]{2,1,0:T(8,128)(2,1)}, bf16[8,128,256]{2,1,0:T(8,128)(2,1)}, u32[]{:S(2)}, u32[]{:S(2)}) %collective-permute-start.7) | collective-permute-done | bytes 524320 | tf_op jit(solution)/shard_map/ppermute | solution.py:18
  135.2 1.1 slice.47
  136.2 0.9 bitcast_dynamic-update-slice_fusion.6
  137.1 0.9 bitcast_dynamic-update-slice_fusion.5
  138.0 0.9 bitcast_dynamic-update-slice_fusion.4
  139.0 0.9 bitcast_dynamic-update-slice_fusion.3
  139.9 0.9 bitcast_dynamic-update-slice_fusion.2
  140.8 0.9 bitcast_dynamic-update-slice_fusion.1
  141.8 0.9 bitcast_dynamic-update-slice_fusion
  142.7 0.9 bitcast_dynamic-update-slice_fusion.8
  143.6 4.8 fusion
  148.4 5.0 fusion.1
  153.4 1.5 copy-done
  154.9 9.7 %fusion.10 = bf16[8,128,1,4,128]{1,4,3,0,2:T(8,128)(2,1)S(1)} fusion(f32[8,9,128,128,4]{3,2,4,1,0:T(8,128)} %copy-done, f32[8,4,128]{2,1,0:T(4,128)S(1)} %get-tuple-element.5, pred[8,128,9,128]{1,3,2,0:T(8,128)(4,1)S(1)} %broadcast_and_fusion, bf16[9,8,128,256]{3,2,0,1:T(8,128)(2,1)} %bitcast_dynamic-update-slice_fusion.8, f32[8,128,4]{1,2,0:T(4,128)S(1)} %bitcast.162), kind=kOutput, calls=%fused_computation.20 | convolution fusion | flops 1232601088 | bytes 23494656 | tf_op jit(solution)/shard_map/sgrtdu,dsugh->stgrh/dot_general | solution.py:110
  164.6 0.7 copy.106
  165.3 9.0 %convolution_convert_fusion.1 = bf16[1024,4096]{1,0:T(8,128)(2,1)} fusion(bf16[512,4096]{1,0:T(8,128)(2,1)} %all-gather.2.cloned.1.call-done, bf16[64,8,8,128]{3,2,1,0:T(8,128)(2,1)S(1)} %bitcast.159), kind=kOutput, calls=%fused_computation.9 | convolution fusion | flops 4299161600 | bytes 13631488 | tf_op jit(solution)/shard_map/dot_general | solution.py:116
  174.4 85.9 %reduce-scatter.5.cloned.1.call-done = bf16[256,4096]{1,0:T(8,128)(2,1)} async-done(((bf16[1024,4096]{1,0:T(8,128)(2,1)}), bf16[256,4096]{1,0:T(8,128)(2,1)}) %reduce-scatter.5.cloned.1.call-update) | async-done | bytes 2097168 | tf_op jit(solution)/shard_map/reduce_scatter | solution.py:24
  260.5 0.3 reduce_window_sum.11
  260.8 36.1 %reduce-scatter.7.cloned.1.call-done = bf16[128,4096]{1,0:T(8,128)(2,1)} async-done(((bf16[256,4096]{1,0:T(8,128)(2,1)}), bf16[128,4096]{1,0:T(8,128)(2,1)}) %reduce-scatter.7.cloned.1.call-update) | async-done | bytes 1048592 | tf_op jit(solution)/shard_map/reduce_scatter | solution.py:24
  296.9 1.6 multiply_reduce_fusion
  298.6 1.8 convolution_convert_fusion.2
  300.4 1.3 stack.59
  301.7 125.7 %all_to_all.50 = bf16[16,2,40,4096]{3,2,1,0:T(8,128)(2,1)} all-to-all(bf16[16,2,40,4096]{3,2,1,0:T(8,128)(2,1)S(1)} %stack.59), channel_id=1, replica_groups=mesh['sp_0'=4,'sp_1'=2,'ep_0'=4,'ep_1'=2,'ep_2'=2] {'ep_0','ep_1','ep_2'}, dimensions={0} | all-to-all | bytes 20971520 | tf_op jit(solution)/shard_map/all_to_all | solution.py:135
  427.4 9.6 %copy.107 = bf16[2,16,40,4096]{3,2,1,0:T(8,128)(2,1)} copy(bf16[2,16,40,4096]{3,2,0,1:T(8,128)(2,1)} %bitcast.151) | data formatting | bytes 20971520 | tf_op jit(solution)/shard_map/reshape | solution.py:135
  437.0 13.5 %fusion.35 = f32[2,640,448]{1,2,0:T(8,128)S(1)} fusion(bf16[2,640,4096]{2,1,0:T(8,128)(2,1)} %bitcast.152, bf16[2,448,4096]{2,1,0:T(8,128)(2,1)} %param.21), kind=kOutput, calls=%fused_computation.63 | convolution fusion | flops 4697620480 | bytes 20119552 | tf_op jit(solution)/shard_map/wnd,wfd->wnf/dot_general | solution.py:136
  450.5 12.9 %multiply_convert_fusion = bf16[2,640,448]{1,2,0:T(8,128)(2,1)} fusion(f32[2,640,448]{1,2,0:T(8,128)S(1)} %fusion.35, bf16[2,640,4096]{2,1,0:T(8,128)(2,1)} %bitcast.153, bf16[2,448,4096]{2,1,0:T(8,128)(2,1)} %param.22), kind=kOutput, calls=%fused_computation.18 | convolution fusion | flops 4701061120 | bytes 21266432 | tf_op jit(solution)/shard_map/wnd,wfd->wnf/dot_general | solution.py:139
  463.5 10.6 %convolution_convert_fusion = bf16[2,640,4096]{2,1,0:T(8,128)(2,1)} fusion(bf16[2,640,448]{1,2,0:T(8,128)(2,1)} %multiply_convert_fusion, bf16[2,448,4096]{2,1,0:T(8,128)(2,1)} %param.23), kind=kOutput, calls=%fused_computation.8 | convolution fusion | flops 4702863360 | bytes 18972672 | tf_op jit(solution)/shard_map/wnf,wfd->wnd/dot_general | solution.py:141
  474.1 9.5 %copy.108 = bf16[8,2,2,40,4096]{4,3,2,0,1:T(8,128)(2,1)} copy(bf16[8,2,2,40,4096]{4,3,1,0,2:T(8,128)(2,1)} %bitcast.154) | data formatting | bytes 20971520 | tf_op jit(solution)/shard_map/reshape | solution.py:37
  483.6 0.0 reduce-scatter.11.cloned.1.call-start
  483.6 17.7 %reduce-scatter.9.cloned.1.call-done = bf16[8,2,40,4096]{3,2,1,0:T(8,128)(2,1)} async-done(((bf16[16,2,40,4096]{3,2,1,0:T(8,128)(2,1)}), bf16[8,2,40,4096]{3,2,1,0:T(8,128)(2,1)}) %reduce-scatter.9.cloned.1.call-update) | async-done | bytes 5242896 | tf_op jit(solution)/shard_map/reduce_scatter | solution.py:38
  501.4 95.9 %reduce-scatter.11.cloned.1.call-done = bf16[1,2,40,4096]{3,2,1,0:T(8,128)(2,1)} async-done(((bf16[8,2,40,4096]{3,2,1,0:T(8,128)(2,1)}), bf16[1,2,40,4096]{3,2,1,0:T(8,128)(2,1)}) %reduce-scatter.11.cloned.1.call-update) | async-done | bytes 655376 | tf_op jit(solution)/shard_map/reduce_scatter | solution.py:39
  597.4 3.2 fusion.8
  (39 shorter events, 0.5 us)
Async XLA Ops:
  8.5 12.6 %all-to-all-start = ((bf16[1,128,8,128]{3,1,0,2:T(8,128)(2,1)}), bf16[1,128,8,128]{3,1,0,2:T(8,128)(2,1)S(1)}, u32[]{:S(2)}, u32[]{:S(2)}) async-start(bf16[1,128,8,128]{3,1,0,2:T(8,128)(2,1)} %copy.90), calls=%async_computation | async-start | bytes 524288 | tf_op jit(solution)/shard_map/all_to_all | solution.py:75
  21.2 10.3 %all-to-all-start.1 = ((bf16[1,128,8,128]{3,1,0,2:T(8,128)(2,1)}), bf16[1,128,8,128]{3,1,0,2:T(8,128)(2,1)S(1)}, u32[]{:S(2)}, u32[]{:S(2)}) async-start(bf16[1,128,8,128]{3,1,0,2:T(8,128)(2,1)} %copy.92), calls=%async_computation.1 | async-start | bytes 524288 | tf_op jit(solution)/shard_map/all_to_all | solution.py:76
  24.6 140.7 %all-gather.2.cloned.1.call-start = ((), (), s32[]{:S(2)}) async-start(), calls=%async_computation.8 | async-start | bytes 4456448 | tf_op jit(solution)/shard_map/all_gather | solution.py:115
  31.4 112.2 %all-to-all-start.2 = ((bf16[1,128,8,512]{1,3,0,2:T(8,128)(2,1)}), bf16[1,128,8,512]{1,3,0,2:T(8,128)(2,1)}, u32[]{:S(2)}, u32[]{:S(2)}) async-start(bf16[1,128,8,512]{1,3,0,2:T(8,128)(2,1)} %bitcast.29), calls=%async_computation.2 | async-start | bytes 2097152 | tf_op jit(solution)/shard_map/all_to_all | solution.py:74
  35.7 224.7 %reduce-scatter.5.cloned.1.call-start = ((), (), s32[]{:S(2)}) async-start(), calls=%async_computation.9 | async-start | bytes 10485760 | tf_op jit(solution)/shard_map/reduce_scatter | solution.py:24
  36.6 27.8 %collective-permute-start = (bf16[8,128,256]{2,1,0:T(8,128)(2,1)}, bf16[8,128,256]{2,1,0:T(8,128)(2,1)S(1)}, u32[]{:S(2)}, u32[]{:S(2)}) collective-permute-start(bf16[8,128,256]{2,1,0:T(8,128)(2,1)} %pad_maximum_fusion), channel_id=1, source_target_pairs={{0,1},{1,2},{2,3},{3,4},{4,5},{5,6},{6,7},{7,8},{8,9},{9,10},{10,1... | collective-permute-start | bytes 1572872 | tf_op jit(solution)/shard_map/ppermute | solution.py:18
  36.6 30.1 %collective-permute-start.1 = (bf16[8,128,256]{2,1,0:T(8,128)(2,1)}, bf16[8,128,256]{2,1,0:T(8,128)(2,1)S(1)}, u32[]{:S(2)}, u32[]{:S(2)}) collective-permute-start(bf16[8,128,256]{2,1,0:T(8,128)(2,1)} %pad_maximum_fusion), channel_id=1, source_target_pairs={{0,2},{1,3},{2,4},{3,5},{4,6},{5,7},{6,8},{7,9},{8,10},{9,11},{10,... | collective-permute-start | bytes 1572872 | tf_op jit(solution)/shard_map/ppermute | solution.py:18
  39.5 61.2 %collective-permute-start.2 = (bf16[8,128,256]{2,1,0:T(8,128)(2,1)}, bf16[8,128,256]{2,1,0:T(8,128)(2,1)S(1)}, u32[]{:S(2)}, u32[]{:S(2)}) collective-permute-start(bf16[8,128,256]{2,1,0:T(8,128)(2,1)} %pad_maximum_fusion), channel_id=1, source_target_pairs={{0,3},{1,4},{2,5},{3,6},{4,7},{5,8},{6,9},{7,10},{8,11},{9,12},{10... | collective-permute-start | bytes 1572872 | tf_op jit(solution)/shard_map/ppermute | solution.py:18
  44.2 63.6 %collective-permute-start.3 = (bf16[8,128,256]{2,1,0:T(8,128)(2,1)}, bf16[8,128,256]{2,1,0:T(8,128)(2,1)}, u32[]{:S(2)}, u32[]{:S(2)}) collective-permute-start(bf16[8,128,256]{2,1,0:T(8,128)(2,1)} %pad_maximum_fusion), channel_id=1, source_target_pairs={{0,4},{1,5},{2,6},{3,7},{4,8},{5,9},{6,10},{7,11},{8,12},{9,13},{1... | collective-permute-start | bytes 1572872 | tf_op jit(solution)/shard_map/ppermute | solution.py:18
  46.2 70.8 %collective-permute-start.4 = (bf16[8,128,256]{2,1,0:T(8,128)(2,1)}, bf16[8,128,256]{2,1,0:T(8,128)(2,1)}, u32[]{:S(2)}, u32[]{:S(2)}) collective-permute-start(bf16[8,128,256]{2,1,0:T(8,128)(2,1)} %pad_maximum_fusion), channel_id=1, source_target_pairs={{0,5},{1,6},{2,7},{3,8},{4,9},{5,10},{6,11},{7,12},{8,13},{9,14},{... | collective-permute-start | bytes 1572872 | tf_op jit(solution)/shard_map/ppermute | solution.py:18
  64.4 53.6 %collective-permute-start.5 = (bf16[8,128,256]{2,1,0:T(8,128)(2,1)}, bf16[8,128,256]{2,1,0:T(8,128)(2,1)}, u32[]{:S(2)}, u32[]{:S(2)}) collective-permute-start(bf16[8,128,256]{2,1,0:T(8,128)(2,1)} %pad_maximum_fusion), channel_id=1, source_target_pairs={{0,6},{1,7},{2,8},{3,9},{4,10},{5,11},{6,12},{7,13},{8,14},{9,15},... | collective-permute-start | bytes 1572872 | tf_op jit(solution)/shard_map/ppermute | solution.py:18
  66.7 57.7 %collective-permute-start.6 = (bf16[8,128,256]{2,1,0:T(8,128)(2,1)}, bf16[8,128,256]{2,1,0:T(8,128)(2,1)}, u32[]{:S(2)}, u32[]{:S(2)}) collective-permute-start(bf16[8,128,256]{2,1,0:T(8,128)(2,1)} %pad_maximum_fusion), channel_id=1, source_target_pairs={{0,7},{1,8},{2,9},{3,10},{4,11},{5,12},{6,13},{7,14},{8,15},{9,0},... | collective-permute-start | bytes 1572872 | tf_op jit(solution)/shard_map/ppermute | solution.py:18
  100.7 34.5 %collective-permute-start.7 = (bf16[8,128,256]{2,1,0:T(8,128)(2,1)}, bf16[8,128,256]{2,1,0:T(8,128)(2,1)}, u32[]{:S(2)}, u32[]{:S(2)}) collective-permute-start(bf16[8,128,256]{2,1,0:T(8,128)(2,1)} %pad_maximum_fusion), channel_id=1, source_target_pairs={{0,8},{1,9},{2,10},{3,11},{4,12},{5,13},{6,14},{7,15},{8,0},{9,1},... | collective-permute-start | bytes 1572872 | tf_op jit(solution)/shard_map/ppermute | solution.py:18
  148.4 6.5 %copy-start = (f32[8,9,128,128,4]{3,2,4,1,0:T(8,128)}, f32[8,9,128,128,4]{3,2,4,1,0:T(8,128)S(1)}, u32[]{:S(2)}) copy-start(f32[8,9,128,128,4]{3,2,4,1,0:T(8,128)S(1)} %get-tuple-element.6) | copy-start | bytes 56623108
  174.3 86.1 %copy-start.5 = (s32[128,2]{0,1:T(2,128)S(1)}, s32[128,2]{0,1:T(2,128)}, u32[]{:S(2)}) copy-start(s32[128,2]{0,1:T(2,128)} %param.19) | copy-start | bytes 3076
  174.3 122.6 %copy-start.1 = (bf16[128,4096]{1,0:T(8,128)(2,1)S(1)}, bf16[128,4096]{1,0:T(8,128)(2,1)}, u32[]{:S(2)}) copy-start(bf16[128,4096]{1,0:T(8,128)(2,1)} %param.12) | copy-start | bytes 3145732
  174.3 124.2 %copy-start.4 = (f32[4096]{0:T(1024)S(1)}, f32[4096]{0:T(1024)}, u32[]{:S(2)}) copy-start(f32[4096]{0:T(1024)} %param.18) | copy-start | bytes 49156
  174.4 122.6 %reduce-scatter.7.cloned.1.call-start = ((), (), s32[]{:S(2)}) async-start(), calls=%async_computation.10 | async-start | bytes 3145728 | tf_op jit(solution)/shard_map/reduce_scatter | solution.py:24
  260.4 241.0 %reduce-scatter.9.cloned.1.call-start = ((), (), s32[]{:S(2)}) async-start(), calls=%async_computation.11 | async-start | bytes 15728640 | tf_op jit(solution)/shard_map/reduce_scatter | solution.py:38
  483.6 17.9 %copy-start.6 = (f32[128,2]{0,1:T(2,128)S(1)}, f32[128,2]{0,1:T(2,128)}, u32[]{:S(2)}) copy-start(f32[128,2]{0,1:T(2,128)} %param.20) | copy-start | bytes 3076
  483.6 113.8 %copy-start.2 = (bf16[128,4096]{1,0:T(8,128)(2,1)S(1)}, bf16[128,4096]{1,0:T(8,128)(2,1)}, u32[]{:S(2)}) copy-start(bf16[128,4096]{1,0:T(8,128)(2,1)} %param.12) | copy-start | bytes 3145732
  483.6 113.8 %copy-start.3 = (bf16[128,4096]{1,0:T(8,128)(2,1)S(1)}, bf16[128,4096]{1,0:T(8,128)(2,1)}, u32[]{:S(2)}) copy-start(bf16[128,4096]{1,0:T(8,128)(2,1)} %reduce-scatter.7.cloned.1.call-done) | copy-start | bytes 3145732
  483.6 113.8 %reduce-scatter.11.cloned.1.call-start = ((), (), s32[]{:S(2)}) async-start(), calls=%async_computation.12 | async-start | bytes 5898240 | tf_op jit(solution)/shard_map/reduce_scatter | solution.py:39
Sparse Core Ops, SparseCore 0:
  27.8 117.8 all-gather.1
  174.5 85.8 reduce-scatter.4
  262.7 34.1 reduce-scatter.6
  483.7 17.6 reduce-scatter.8
  505.1 92.2 reduce-scatter.10
